TPU v7x, 32 devices: a whole 2x2x4 slice. The times are simulated.
32 devices in a mesh: row: 8 (over z, x), col: 4 (over y, core).
Axes of the slice: x: 2, y: 2, z: 4, core: 2. Of those that a mesh axis runs over, the one named last changes fastest.
Arguments:
- matrix: float32 [5, 8, 10, 4, 128, 128], P(None, 'row', None, 'col'), may hold values from 0 to 2.5, as said below
- flags: int32 [5, 8, 10, 4], P(None, 'row', None, 'col'), may hold values from 0 to 1, as said below
Outputs:
- factor: float32 [5, 8, 10, 4, 128, 128], P(None, 'row', None, 'col')
Inputs may be any that keep to these rules, and one draw needn't show every extreme that they name: `matrix`: symmetric positive definite, of order 40*128, diagonal at least 1.5. `flags`: 0 marks a float32 tile, 1 a bfloat16 tile; every diagonal tile is 0.
All inputs are finite; a program needn't handle non-finite values.
Results may differ from a plain program's by a relative error of at most 0.0005.
The roundings to bfloat16 on the way count: a program that leaves them out, or rounds other values in their place, can miss the bound.
Values sent between devices are 32-bit elements; how exact they have to be, the bound alone decides.
A program may use at most 128 MiB of HBM per device.

v0:
```python
import jax
import jax.numpy as jnp
from jax import lax
from jax.sharding import PartitionSpec as P

PT = 4


def spread(value, axis, source):
    kept = jnp.where(lax.axis_index(axis) == source, value, 0).astype(value.dtype)
    return lax.psum(kept, axis)


def storage_round(values):
    narrow = lax.optimization_barrier(values.astype(jnp.bfloat16))
    return narrow.astype(jnp.float32)


def solve_rows(lower_block, rows):
    width = rows.shape[2]
    flat = rows.reshape(-1, width)
    solved = jax.scipy.linalg.solve_triangular(lower_block, flat.T, lower=True).T
    return solved.reshape(rows.shape)


def with_block(solved, lower_block, global_ids, start):
    offset = jnp.clip(global_ids - start, 0, PT - 1)
    block_rows = lower_block.reshape(PT, solved.shape[1], solved.shape[2])[offset]
    inside = (global_ids >= start) & (global_ids < start + PT)
    return jnp.where(inside[:, None, None], block_rows, solved)


def factor_panel(work, start, row_ids, row_count, col_count):
    pieces = []
    for column in range(start, start + PT):
        pieces.append(spread(work[:, column // col_count], "col", column % col_count))
    panel_rows = jnp.concatenate(pieces, axis=2)
    blocks = []
    for tile_row in range(start, start + PT):
        blocks.append(spread(panel_rows[tile_row // row_count], "row", tile_row % row_count))
    dense = jnp.concatenate(blocks, axis=0)
    sym = jnp.tril(dense) + jnp.tril(dense, -1).T
    lower_block = jnp.linalg.cholesky(sym)
    solved = with_block(solve_rows(lower_block, panel_rows), lower_block, row_ids, start)
    return (panel_rows, lower_block, solved)


def apply_update(work, marks, left, right, row_ids, col_ids, low, high):
    exact = jnp.einsum("aik,cjk->acij", left, right, precision=lax.Precision.HIGHEST)
    coarse = jnp.einsum(
        "aik,cjk->acij",
        left.astype(jnp.bfloat16),
        right.astype(jnp.bfloat16),
        preferred_element_type=jnp.float32,
    )
    live = (
        (row_ids[:, None] >= col_ids[None, :])
        & (col_ids >= low)[None, :]
        & (col_ids < high)[None, :]
    )
    updated = jnp.where((marks == 1)[:, :, None, None], work - coarse, work - exact)
    return jnp.where(live[:, :, None, None], updated, work)


def store_panel(work, solved, start, row_ids, col_index, col_count):
    tile = work.shape[2]
    for column in range(start, start + PT):
        slot = column // col_count
        offset = column - start
        piece = solved[:, :, offset * tile : (offset + 1) * tile]
        keep = (row_ids >= start)[:, None, None] & (col_index == column % col_count)
        work = work.at[:, slot].set(jnp.where(keep, piece, work[:, slot]))
    return work


def on_device(matrix, flags):
    row_count = lax.axis_size("row")
    col_count = lax.axis_size("col")
    row_index = lax.axis_index("row")
    col_index = lax.axis_index("col")
    tile_rows = matrix.shape[0]
    tile_cols = matrix.shape[2]
    tile = matrix.shape[4]
    tiles = matrix.reshape(tile_rows, tile_cols, tile, tile)
    marks = flags.reshape(tile_rows, tile_cols)
    row_ids = jnp.arange(tile_rows, dtype=jnp.int32) * row_count + row_index
    col_ids = jnp.arange(tile_cols, dtype=jnp.int32) * col_count + col_index
    work = jnp.where((marks == 1)[:, :, None, None], storage_round(tiles), tiles)
    beyond = 1 << 30
    lefts = []
    rights = []
    for step in range(2):
        start = step * PT
        panel_rows, lower_block, solved = factor_panel(work, start, row_ids, row_count, col_count)
        received = []
        for slot in range(tile_cols):
            column = col_ids[slot]
            piece = lax.dynamic_index_in_dim(solved, column // row_count, 0, keepdims=False)
            received.append(spread(piece, "row", column % row_count))
        right = jnp.stack(received, axis=0)
        lefts.append(solved)
        rights.append(right)
        work = apply_update(work, marks, solved, right, row_ids, col_ids, start + PT, beyond)
        work = store_panel(work, solved, start, row_ids, col_index, col_count)
    final = jnp.where((marks == 1)[:, :, None, None], storage_round(work), work)
    upper = row_ids[:, None] < col_ids[None, :]
    final = jnp.where(upper[:, :, None, None], jnp.float32(0.0), final)
    return final.reshape(matrix.shape)


def solution(mesh):
    return jax.shard_map(
        on_device,
        mesh=mesh,
        in_specs=(P(None, "row", None, "col", None, None), P(None, "row", None, "col")),
        out_specs=P(None, "row", None, "col", None, None),
        check_vma=False,
    )
```

profile of v0, /device:TPU:0, one launch (start us, length us, event | category | flops | bytes accessed | tf_op | source)
XLA Modules:
  0.0 841.9 jit_solution(16314671458284499943)
XLA Ops:
  7.5 2.2 copy.42
  10.1 1.7 copy-done.2
  13.0 42.1 %all-reduce.24.cloned.1.call-done = (f32[5,128,128]{2,1,0:T(8,128)}, f32[5,128,128]{2,1,0:T(8,128)}, f32[5,128,128]{2,1,0:T(8,128)}, f32[5,128,128]{2,1,0:T(8,128)}) async-done(((f32[5,128,128]{2,1,0:T(8,128)}, f32[5,128,128]{2,1,0:T(8,128)}, f32[5,128,128]{2,1,0:T(8,128)}, f32[5,128,128]{2,1,0:T(8,128)}), (f32[5,128,128]{2,1,0:T(8,128)}, f32[5,128,128]{2,1,0:T(8,128)}, f32[5,128,128]{2,1,0:T(8,128)}, ...) | async-done | bytes 1310736 | tf_op jit(solution)/shard_map/psum | solution.py:11
  87.3 52.5 %all-reduce.20.cloned.1.call-done = (f32[128,512]{1,0:T(8,128)}, f32[128,512]{1,0:T(8,128)}, f32[128,512]{1,0:T(8,128)}, f32[128,512]{1,0:T(8,128)}) async-done(((f32[128,512]{1,0:T(8,128)}, f32[128,512]{1,0:T(8,128)}, f32[128,512]{1,0:T(8,128)}, f32[128,512]{1,0:T(8,128)}), (f32[128,512]{1,0:T(8,128)}, f32[128,512]{1,0:T(8,128)}, f32[128,512]{1,0:T(8,128)}, ...) | async-done | bytes 1048592 | tf_op jit(solution)/shard_map/psum | solution.py:11
  144.8 11.7 %cholesky.286 = f32[128,128]{1,0:T(8,128)S(1)} custom-call(f32[128,128]{1,0:T(8,128)S(1)} %cholesky.426), custom_call_target="Cholesky" | custom-call | tf_op jit(solution)/shard_map/jit(cholesky)/cholesky | solution.py:43
  156.7 9.8 %custom-call.27 = f32[1,128,128]{1,2,0:T(8,128)S(1)} custom-call(f32[1,128,128]{2,1,0:T(8,128)S(1)} %get-tuple-element.236), custom_call_target="InvertDiagBlocksLowerTriangular" | custom-call | tf_op jit(solution)/shard_map/jit(cholesky)/cholesky | solution.py:43
  167.2 11.7 %cholesky.305 = f32[128,128]{1,0:T(8,128)S(1)} custom-call(f32[128,128]{1,0:T(8,128)S(1)} %cholesky.430), custom_call_target="Cholesky" | custom-call | tf_op jit(solution)/shard_map/jit(cholesky)/cholesky | solution.py:43
  179.0 9.9 %custom-call.28 = f32[1,128,128]{1,2,0:T(8,128)S(1)} custom-call(f32[1,128,128]{2,1,0:T(8,128)S(1)} %get-tuple-element.233), custom_call_target="InvertDiagBlocksLowerTriangular" | custom-call | tf_op jit(solution)/shard_map/jit(cholesky)/cholesky | solution.py:43
  189.5 11.7 %cholesky.326 = f32[128,128]{1,0:T(8,128)S(1)} custom-call(f32[128,128]{1,0:T(8,128)S(1)} %cholesky.435), custom_call_target="Cholesky" | custom-call | tf_op jit(solution)/shard_map/jit(cholesky)/cholesky | solution.py:43
  202.0 9.8 %custom-call.29 = f32[1,128,128]{1,2,0:T(8,128)S(1)} custom-call(f32[1,128,128]{2,1,0:T(8,128)S(1)} %get-tuple-element.230), custom_call_target="InvertDiagBlocksLowerTriangular" | custom-call | tf_op jit(solution)/shard_map/jit(cholesky)/cholesky | solution.py:43
  212.4 11.9 %cholesky.343 = f32[128,128]{1,0:T(8,128)S(1)} custom-call(f32[128,128]{1,0:T(8,128)S(1)} %convolution_subtract_fusion.11), custom_call_target="Cholesky" | custom-call | tf_op jit(solution)/shard_map/jit(cholesky)/cholesky | solution.py:43
  228.6 8.1 while.12
  229.3 1.3 bitcast_dynamic-update-slice_fusion.10
  231.3 1.3 bitcast_dynamic-update-slice_fusion.10
  236.7 39.3 %custom-call.30 = f32[4,128,128]{1,2,0:T(8,128)S(1)} custom-call(f32[4,128,128]{2,1,0:T(8,128)S(1)} %get-tuple-element.117), custom_call_target="InvertDiagBlocksLowerTriangular" | custom-call | tf_op jit(solution)/shard_map/jit(_solve_triangular)/triangular_solve | solution.py:22
  276.0 1.5 fusion.46
  277.5 1.7 convolution_subtract_fusion.3
  279.7 2.2 convolution_subtract_fusion.2
  282.4 2.7 convolution_subtract_fusion.5
  286.8 1.7 copy.9
  288.5 1.7 gather_fusion
  290.3 1.6 broadcast_select_fusion.1
  292.6 1.5 dynamic-slice_select_fusion.10
  294.8 115.8 %all-reduce.18.cloned.1.call-done = (f32[1,128,512]{2,1,0:T(8,128)}, f32[1,128,512]{2,1,0:T(8,128)}, f32[1,128,512]{2,1,0:T(8,128)}, f32[1,128,512]{2,1,0:T(8,12...) async-done(((f32[1,128,512]{2,1,0:T(8,128)}, ...) | async-done | bytes 2621456 | tf_op jit(solution)/shard_map/psum | solution.py:11
  415.8 5.4 fusion.6
  423.0 1.7 copy-done
  425.9 38.2 %all-reduce.22.cloned.1.call-done = (f32[5,128,128]{2,1,0:T(8,128)}, f32[5,128,128]{2,1,0:T(8,128)}, f32[5,128,128]{2,1,0:T(8,128)}, f32[5,128,128]{2,1,0:T(8,128)}) async-done(((f32[5,128,128]{2,1,0:T(8,128)}, f32[5,128,128]{2,1,0:T(8,128)}, f32[5,128,128]{2,1,0:T(8,128)}, f32[5,128,128]{2,1,0:T(8,128)}), (f32[5,128,128]{2,1,0:T(8,128)}, f32[5,128,128]{2,1,0:T(8,128)}, f32[5,128,128]{2,1,0:T(8,128)}, ...) | async-done | bytes 1310736 | tf_op jit(solution)/shard_map/psum | solution.py:11
  471.0 77.9 %all-reduce.16.cloned.1.call-done = (f32[128,512]{1,0:T(8,128)}, f32[128,512]{1,0:T(8,128)}, f32[128,512]{1,0:T(8,128)}, f32[128,512]{1,0:T(8,128)}) async-done(((f32[128,512]{1,0:T(8,128)}, f32[128,512]{1,0:T(8,128)}, f32[128,512]{1,0:T(8,128)}, f32[128,512]{1,0:T(8,128)}), (f32[128,512]{1,0:T(8,128)}, f32[128,512]{1,0:T(8,128)}, f32[128,512]{1,0:T(8,128)}, ...) | async-done | bytes 1048592 | tf_op jit(solution)/shard_map/psum | solution.py:11
  554.0 11.7 %cholesky.358 = f32[128,128]{1,0:T(8,128)S(1)} custom-call(f32[128,128]{1,0:T(8,128)S(1)} %cholesky.439), custom_call_target="Cholesky" | custom-call | tf_op jit(solution)/shard_map/jit(cholesky)/cholesky | solution.py:43
  565.9 9.8 %custom-call.31 = f32[1,128,128]{1,2,0:T(8,128)S(1)} custom-call(f32[1,128,128]{2,1,0:T(8,128)S(1)} %get-tuple-element.226), custom_call_target="InvertDiagBlocksLowerTriangular" | custom-call | tf_op jit(solution)/shard_map/jit(cholesky)/cholesky | solution.py:43
  576.4 11.7 %cholesky.377 = f32[128,128]{1,0:T(8,128)S(1)} custom-call(f32[128,128]{1,0:T(8,128)S(1)} %cholesky.443), custom_call_target="Cholesky" | custom-call | tf_op jit(solution)/shard_map/jit(cholesky)/cholesky | solution.py:43
  589.8 9.8 %custom-call.32 = f32[1,128,128]{1,2,0:T(8,128)S(1)} custom-call(f32[1,128,128]{2,1,0:T(8,128)S(1)} %get-tuple-element.223), custom_call_target="InvertDiagBlocksLowerTriangular" | custom-call | tf_op jit(solution)/shard_map/jit(cholesky)/cholesky | solution.py:43
  600.3 11.7 %cholesky.398 = f32[128,128]{1,0:T(8,128)S(1)} custom-call(f32[128,128]{1,0:T(8,128)S(1)} %cholesky.448), custom_call_target="Cholesky" | custom-call | tf_op jit(solution)/shard_map/jit(cholesky)/cholesky | solution.py:43
  612.7 9.8 %custom-call.33 = f32[1,128,128]{1,2,0:T(8,128)S(1)} custom-call(f32[1,128,128]{2,1,0:T(8,128)S(1)} %get-tuple-element.220), custom_call_target="InvertDiagBlocksLowerTriangular" | custom-call | tf_op jit(solution)/shard_map/jit(cholesky)/cholesky | solution.py:43
  623.1 11.9 %cholesky.415 = f32[128,128]{1,0:T(8,128)S(1)} custom-call(f32[128,128]{1,0:T(8,128)S(1)} %convolution_subtract_fusion.10), custom_call_target="Cholesky" | custom-call | tf_op jit(solution)/shard_map/jit(cholesky)/cholesky | solution.py:43
  638.4 7.3 while.13
  645.7 39.3 %custom-call.34 = f32[4,128,128]{1,2,0:T(8,128)S(1)} custom-call(f32[4,128,128]{2,1,0:T(8,128)S(1)} %get-tuple-element.118), custom_call_target="InvertDiagBlocksLowerTriangular" | custom-call | tf_op jit(solution)/shard_map/jit(_solve_triangular)/triangular_solve | solution.py:22
  685.0 1.5 fusion.41
  686.5 1.7 convolution_subtract_fusion.1
  688.7 2.2 convolution_subtract_fusion
  691.4 2.7 convolution_subtract_fusion.4
  695.8 1.7 copy.15
  697.5 1.7 gather_fusion.1
  699.2 1.6 broadcast_select_fusion
  700.9 1.5 dynamic-slice_select_fusion
  703.2 116.4 %all-reduce.14.cloned.1.call-done = (f32[1,128,512]{2,1,0:T(8,128)}, f32[1,128,512]{2,1,0:T(8,128)}, f32[1,128,512]{2,1,0:T(8,128)}, f32[1,128,512]{2,1,0:T(8,12...) async-done(((f32[1,128,512]{2,1,0:T(8,128)}, ...) | async-done | bytes 2621456 | tf_op jit(solution)/shard_map/psum | solution.py:11
  824.8 5.6 fusion.4
  832.9 1.9 copy.18
  (202 shorter events, 71.8 us)
Async XLA Ops:
  6.5 3.2 copy-start.4
  6.5 48.5 %all-reduce.24.cloned.1.call-start = ((), (), s32[]{:S(2)}) async-start(), calls=%async_computation.5 | async-start | bytes 2621440 | tf_op jit(solution)/shard_map/psum | solution.py:11
  10.1 1.7 copy-start.2
  12.9 126.9 %all-reduce.20.cloned.1.call-start = ((), (), s32[]{:S(2)}) async-start(), calls=%async_computation.3 | async-start | bytes 2097152 | tf_op jit(solution)/shard_map/psum | solution.py:11
  59.1 1.1 copy-start.5
  61.3 349.3 %all-reduce.18.cloned.1.call-start = ((), (), s32[]{:S(2)}) async-start(), calls=%async_computation.2 | async-start | bytes 5242880 | tf_op jit(solution)/shard_map/psum | solution.py:11
  294.1 169.9 %all-reduce.22.cloned.1.call-start = ((), (), s32[]{:S(2)}) async-start(), calls=%async_computation.4 | async-start | bytes 2621440 | tf_op jit(solution)/shard_map/psum | solution.py:11
  410.6 5.0 copy-start.11
  410.6 5.0 copy-start.10
  410.6 5.1 copy-start.9
  410.6 5.1 copy-start.8
  410.6 5.1 copy-start.7
  415.8 5.4 copy-start.3
  423.0 1.7 copy-start
  425.8 123.0 %all-reduce.16.cloned.1.call-start = ((), (), s32[]{:S(2)}) async-start(), calls=%async_computation.1 | async-start | bytes 2097152 | tf_op jit(solution)/shard_map/psum | solution.py:11
  468.1 1.1 copy-start.6
  470.2 349.3 %all-reduce.14.cloned.1.call-start = ((), (), s32[]{:S(2)}) async-start(), calls=%async_computation | async-start | bytes 5242880 | tf_op jit(solution)/shard_map/psum | solution.py:11
  819.6 5.0 copy-start.16
  819.6 5.0 copy-start.15
  819.6 5.1 copy-start.14
  819.6 5.1 copy-start.13
  819.6 5.1 copy-start.12
  824.7 5.6 copy-start.1
Sparse Core Ops, SparseCore 0:
  13.0 41.9 all-reduce.23
  61.4 78.4 all-reduce.19
  294.3 116.2 all-reduce.17
  425.9 38.0 all-reduce.21
  470.4 78.4 all-reduce.15
  703.2 116.2 all-reduce.13
where the time goes:
time: 853 us; the launch traced here: 842 us
  waiting for transfers between devices  443 us (52%)
  other arithmetic  256 us (30%)
  local copies, waits for them, and re-layouts  60.7 us (7%)
  between operations  45 us (5%)
  matrix products  36.4 us (4%)
    psum x6, waiting for transfers between devices, spread(): return lax.psum(kept, axis)  443 us
    another operation x29, other arithmetic, factor_panel(): lower_block = jnp.linalg.cholesky(sym)  158 us
    another operation x5, other arithmetic, solve_rows(): jax.scipy.linalg.solve_triangular(lower_block, flat.T, lower=True)  79.2 us
    unnamed x65, local copies, waits for them, and re-layouts  29.8 us
    another operation x14, matrix products, solve_rows(): jax.scipy.linalg.solve_triangular(lower_block, flat.T, lower=True)  19.1 us
  transfers between devices with their start and end apart: 6, of which 6 were waited for; matrix products, arithmetic and copies ran while one was open for 0% of the time, Pallas kernels for 0%

commit v1 on v0

v1 whole, which is shorter than its diff:
```python
import jax
import jax.numpy as jnp
from jax import lax
from jax.experimental import pallas as pl
from jax.experimental.pallas import tpu as pltpu
from jax.sharding import PartitionSpec as P

PT = 4
MICRO = 8
NT_DIMS = (((1,), (1,)), ((), ()))
TN_DIMS = (((0,), (0,)), ((), ()))


def dot_nt(a, b):
    return lax.dot_general(
        a, b, NT_DIMS, precision=lax.Precision.HIGHEST, preferred_element_type=jnp.float32
    )


def dot_nt_coarse(a, b):
    return lax.dot_general(
        a.astype(jnp.bfloat16),
        b.astype(jnp.bfloat16),
        NT_DIMS,
        preferred_element_type=jnp.float32,
    )


def factor_tile(start, work_ref, low_ref, inv_ref):
    tile = start.shape[0]
    lane = lax.broadcasted_iota(jnp.int32, (tile, tile), 1)
    sub = lax.broadcasted_iota(jnp.int32, (tile, tile), 0)
    work_ref[:, :tile] = start
    work_ref[:, tile:] = (lane == sub).astype(jnp.float32)
    lane8 = lax.broadcasted_iota(jnp.int32, (MICRO, tile), 1)
    sub8 = lax.broadcasted_iota(jnp.int32, (MICRO, tile), 0)

    def micro(p, carry):
        base = pl.multiple_of(p * MICRO, MICRO)
        both = work_ref[pl.ds(base, MICRO), :]
        turned = pltpu.roll(both[:, :tile], lax.rem(tile - base, tile), 1)
        s = {}
        for k in range(MICRO):
            for q in range(k + 1):
                s[k, q] = jnp.broadcast_to(turned[k : k + 1, q : q + 1], (1, 2 * tile))
        rows = [both[k : k + 1, :] for k in range(MICRO)]
        for q in range(MICRO):
            d = s[q, q]
            r = lax.rsqrt(d)
            r = r * (1.5 - 0.5 * d * r * r)
            rows[q] = rows[q] * r
            low = {k: s[k, q] * r for k in range(q + 1, MICRO)}
            for k in range(q + 1, MICRO):
                for m in range(q + 1, k + 1):
                    s[k, m] = s[k, m] - low[k] * low[m]
                rows[k] = rows[k] - low[k] * rows[q]
        done = jnp.concatenate(rows, axis=0)
        upper = jnp.where(lane8 >= base + sub8, done[:, :tile], 0.0)
        extra = done[:, tile:]
        low_ref[pl.ds(base, MICRO), :] = upper
        inv_ref[pl.ds(base, MICRO), :] = extra
        work_ref[...] -= lax.dot_general(
            upper,
            jnp.concatenate([upper, extra], axis=1),
            TN_DIMS,
            precision=lax.Precision.HIGHEST,
            preferred_element_type=jnp.float32,
        )
        return carry

    lax.fori_loop(0, tile // MICRO, micro, 0)


def factor_kernel(col_count, tile, grid_ref, low_ref, inv_ref, work_ref, up_ref):
    count = 2 * PT
    lane = lax.broadcasted_iota(jnp.int32, (tile, tile), 1)
    sub = lax.broadcasted_iota(jnp.int32, (tile, tile), 0)

    def span(i, j=None):
        return slice(i * tile, (i + 1 if j is None else j) * tile)

    for i in range(count):
        for j in range(i + 1):
            piece = grid_ref[i, j % col_count, j // col_count, :tile, :]
            if i == j:
                kept = jnp.where(lane <= sub, piece, 0.0)
                piece = kept + jnp.where(lane < sub, piece, 0.0).T
            low_ref[span(i), span(j)] = piece
        if i + 1 < count:
            low_ref[span(i), span(i + 1, count)] = jnp.zeros(
                (tile, (count - i - 1) * tile), jnp.float32
            )
    for t in range(count):
        stop = PT if t < PT else count
        if t == PT:
            for i in range(PT, count):
                left = low_ref[span(i), span(0, PT)]
                for j in range(PT, i + 1):
                    right = low_ref[span(j), span(0, PT)]
                    mark = grid_ref[i, j % col_count, j // col_count, tile : tile + 1, :]
                    taken = jnp.where(mark > 0.5, dot_nt_coarse(left, right), dot_nt(left, right))
                    low_ref[span(i), span(j)] -= taken
        factor_tile(low_ref[span(t), span(t)], work_ref, up_ref, inv_ref.at[t])
        low_ref[span(t), span(t)] = up_ref[...].T
        if t + 1 < count:
            solved = dot_nt(low_ref[span(t + 1, count), span(t)], inv_ref[t])
            low_ref[span(t + 1, count), span(t)] = solved
            for u in range(t + 1, stop):
                low_ref[span(u, count), span(u)] -= dot_nt(
                    low_ref[span(u, count), span(t)], low_ref[span(u), span(t)]
                )


def factor_blocks(grid):
    col_count = grid.shape[1]
    tile = grid.shape[4]
    count = 2 * PT
    return pl.pallas_call(
        lambda *refs: factor_kernel(col_count, tile, *refs),
        out_shape=(
            jax.ShapeDtypeStruct((count * tile, count * tile), jnp.float32),
            jax.ShapeDtypeStruct((count, tile, tile), jnp.float32),
        ),
        in_specs=[pl.BlockSpec(memory_space=pltpu.VMEM)],
        out_specs=(
            pl.BlockSpec(memory_space=pltpu.VMEM),
            pl.BlockSpec(memory_space=pltpu.VMEM),
        ),
        scratch_shapes=[
            pltpu.VMEM((tile, 2 * tile), jnp.float32),
            pltpu.VMEM((tile, tile), jnp.float32),
        ],
        cost_estimate=pl.CostEstimate(flops=40_000_000_000, bytes_accessed=9_000_000, transcendentals=0),
        name="factor_blocks",
    )(grid)


def solve_kernel(col_count, tile, ids_ref, panel_ref, low_ref, inv_ref, out_ref):
    count = 2 * PT
    row = ids_ref[pl.program_id(0)]

    def span(i, j=None):
        return slice(i * tile, (i + 1 if j is None else j) * tile)

    @pl.when(row < count)
    def _():
        base = pl.multiple_of(jnp.minimum(row, count - 1) * tile, tile)
        out_ref[0] = low_ref[pl.ds(base, tile), :]

    @pl.when(row >= count)
    def _():
        for step in range(2):
            first = step * PT
            if step == 1:
                before = out_ref[0, :, span(0, PT)]
                other = low_ref[span(PT, count), span(0, PT)]
                exact = dot_nt(before, other)
                coarse = dot_nt_coarse(before, other)
            for t in range(first, first + PT):
                value = panel_ref[t % col_count, 0, t // col_count, :tile, :]
                if step == 1:
                    mark = panel_ref[t % col_count, 0, t // col_count, tile : tile + 1, :]
                    value = value - jnp.where(
                        mark > 0.5, coarse[:, span(t - PT)], exact[:, span(t - PT)]
                    )
                if t > first:
                    value = value - dot_nt(
                        out_ref[0, :, span(first, t)], low_ref[span(t), span(first, t)]
                    )
                out_ref[0, :, span(t)] = dot_nt(value, inv_ref[t])


def solve_panels(ids, panels, low, inv, groups):
    col_count = panels.shape[0] // groups
    _, rows, slots, height, tile = panels.shape
    count = 2 * PT
    total = rows * groups
    return pl.pallas_call(
        lambda *refs: solve_kernel(col_count, tile, *refs),
        grid_spec=pltpu.PrefetchScalarGridSpec(
            num_scalar_prefetch=1,
            grid=(total,),
            in_specs=[
                pl.BlockSpec(
                    (col_count, 1, slots, height, tile),
                    lambda g, ids: (g % groups, g // groups, 0, 0, 0),
                ),
                pl.BlockSpec((count * tile, count * tile), lambda g, ids: (0, 0)),
                pl.BlockSpec((count, tile, tile), lambda g, ids: (0, 0, 0)),
            ],
            out_specs=pl.BlockSpec((1, tile, count * tile), lambda g, ids: (g, 0, 0)),
        ),
        out_shape=jax.ShapeDtypeStruct((total, tile, count * tile), jnp.float32),
        cost_estimate=pl.CostEstimate(
            flops=total * 800_000_000, bytes_accessed=total * 1_000_000, transcendentals=0
        ),
        name="solve_panels",
    )(ids, panels, low, inv)


def update_kernel(tile, rows_ref, cols_ref, marks_ref, raw_ref, left_ref, right_ref, out_ref):
    count = 2 * PT
    a = pl.program_id(0)
    b = pl.program_id(1)
    i = rows_ref[a]
    j = cols_ref[b]
    mark = marks_ref[a * pl.num_programs(1) + b]

    def rounded(value):
        return value.astype(jnp.bfloat16).astype(jnp.float32)

    @pl.when(i < j)
    def _():
        out_ref[...] = jnp.zeros_like(out_ref)

    @pl.when((i >= j) & (j < count))
    def _():
        base = pl.multiple_of(jnp.minimum(j, count - 1) * tile, tile)
        value = left_ref[a, :, pl.ds(base, tile)]
        out_ref[0, 0] = jnp.where(mark == 1, rounded(value), value)

    @pl.when((i >= j) & (j >= count) & (mark == 1))
    def _():
        value = rounded(raw_ref[0, 0]) - dot_nt_coarse(left_ref[a], right_ref[b])
        out_ref[0, 0] = rounded(value)

    @pl.when((i >= j) & (j >= count) & (mark != 1))
    def _():
        out_ref[0, 0] = raw_ref[0, 0] - dot_nt(left_ref[a], right_ref[b])


def update_tiles(row_ids, col_ids, marks, tiles, left, right):
    rows, cols, tile, _ = tiles.shape
    whole = lambda a, b, *refs: (0, 0, 0)
    each = lambda a, b, *refs: (a, b, 0, 0)
    return pl.pallas_call(
        lambda *refs: update_kernel(tile, *refs),
        grid_spec=pltpu.PrefetchScalarGridSpec(
            num_scalar_prefetch=3,
            grid=(rows, cols),
            in_specs=[
                pl.BlockSpec((1, 1, tile, tile), each),
                pl.BlockSpec(left.shape, whole),
                pl.BlockSpec(right.shape, whole),
            ],
            out_specs=pl.BlockSpec((1, 1, tile, tile), each),
        ),
        out_shape=jax.ShapeDtypeStruct(tiles.shape, jnp.float32),
        compiler_params=pltpu.CompilerParams(vmem_limit_bytes=60 * 1024 * 1024),
        name="update_tiles",
    )(row_ids, col_ids, marks.reshape(-1), tiles, left, right)


def on_device(matrix, flags):
    row_count = lax.axis_size("row")
    col_count = lax.axis_size("col")
    row_index = lax.axis_index("row")
    col_index = lax.axis_index("col")
    tile_rows = matrix.shape[0]
    tile_cols = matrix.shape[2]
    tile = matrix.shape[4]
    count = 2 * PT
    slots = count // col_count
    groups = row_count // col_count
    tiles = matrix.reshape(tile_rows, tile_cols, tile, tile)
    marks = flags.reshape(tile_rows, tile_cols)
    row_ids = jnp.arange(tile_rows, dtype=jnp.int32) * row_count + row_index
    col_ids = jnp.arange(tile_cols, dtype=jnp.int32) * col_count + col_index

    head = tiles[:, :slots]
    head_marks = (marks[:, :slots] == 1)[:, :, None, None]
    stored = jnp.where(head_marks, lax.reduce_precision(head, 8, 7), head)
    tags = jnp.broadcast_to(head_marks.astype(jnp.float32), (tile_rows, slots, 8, tile))
    payload = jnp.concatenate([stored, tags], axis=2)

    grid = lax.all_gather(payload[0], ("row", "col"))
    grid = grid.reshape(row_count, col_count, slots, tile + 8, tile)[:count]
    low, inv = factor_blocks(grid)

    perm = []
    for h in range(groups):
        for u in range(col_count):
            for v in range(col_count):
                source = (h * col_count + u) * col_count + v
                perm.append((source, (h * col_count + v) * col_count + u))
    swapped = lax.ppermute(payload, ("row", "col"), perm)
    own = lax.all_gather(payload, "col")
    across = lax.all_gather(swapped, "row")

    left = solve_panels(row_ids, own, low, inv, 1)
    right = solve_panels(col_ids, across, low, inv, groups)
    out = update_tiles(row_ids, col_ids, marks, tiles, left, right)
    return out.reshape(matrix.shape)


def solution(mesh):
    return jax.shard_map(
        on_device,
        mesh=mesh,
        in_specs=(P(None, "row", None, "col", None, None), P(None, "row", None, "col")),
        out_specs=P(None, "row", None, "col", None, None),
        check_vma=False,
    )
```

time: 853 us -> 281 us (0.33); the launches traced: 842 us -> 279 us
  waiting for transfers between devices: 443 us -> 70.8 us
  other arithmetic: 256 us -> 3.88 us
  Pallas kernels: 0 us -> 187 us
  local copies, waits for them, and re-layouts: 60.7 us -> 2.38 us
  matrix products: 36.4 us -> 0 us
  between operations: 45 us -> 13.1 us
    psum x6 -> x0, waiting for transfers between devices: 443 us -> none  [spread(): return lax.psum(kept, axis)]
    another operation x34 -> x0, other arithmetic: 238 us -> none  [the longest x29 158 us: factor_panel(): lower_block = jnp.linalg.cholesky(sym)]
    pallas_call x0 -> x4, Pallas kernels: none -> 187 us  [the longest x1 86.8 us: factor_blocks(): pl.pallas_call(lambda *refs: factor_kernel(col_count, tile, *refs), out_s...]
    all_gather x0 -> x3, waiting for transfers between devices: none -> 70.7 us  [the longest x1 62 us: on_device(): grid = lax.all_gather(payload[0], ('row', 'col'))]
    unnamed x65 -> x5, local copies, waits for them, and re-layouts: 29.8 us -> 1.64 us
    another operation x26 -> x0, matrix products: 22.9 us -> none  [the longest x14 19.1 us: solve_rows(): jax.scipy.linalg.solve_triangular(lower_block, flat.T, lower=True)]
    another operation x37 -> x1, local copies, waits for them, and re-layouts: 15.6 us -> 0.67 us  [update_tiles(): marks.reshape(-1)]
    dot_general x4 -> x0, matrix products: 13.6 us -> none  [the longest x2 11 us: apply_update(): jnp.einsum('aik,cjk->acij', left, right, precision=lax.Precision.HIGHEST)]
  transfers between devices with their start and end apart: 6 -> 4, of which waited for: 6 -> 2; matrix products, arithmetic and copies ran while one was open for 0% -> 1% of each run, Pallas kernels for 0% -> 40%
where the time goes in v1:
time: 281 us; the launch traced here: 279 us
  Pallas kernels  187 us (67%)
  waiting for transfers between devices  70.8 us (25%)
  between operations  13.1 us (5%)
  other arithmetic  3.88 us (1%)
    pallas_call x1, Pallas kernels, factor_blocks(): pl.pallas_call(lambda *refs: factor_kernel(col_count, tile, *refs), out_s...  86.8 us
    pallas_call x2, Pallas kernels, solve_panels(): pl.pallas_call(lambda *refs: solve_kernel(col_count, tile, *refs), grid_s...  67.9 us
    all_gather x1, waiting for transfers between devices, on_device(): grid = lax.all_gather(payload[0], ('row', 'col'))  62 us
    pallas_call x1, Pallas kernels, update_tiles(): pl.pallas_call(lambda *refs: update_kernel(tile, *refs), grid_spec=pltpu....  31.8 us
    all_gather x1, waiting for transfers between devices, on_device(): across = lax.all_gather(swapped, 'row')  8.72 us
  transfers between devices with their start and end apart: 4, of which 2 were waited for; matrix products, arithmetic and copies ran while one was open for 1% of the time, Pallas kernels for 40%

profile of v1, /device:TPU:0, one launch (start us, length us, event | category | flops | bytes accessed | tf_op | source)
XLA Modules:
  0.0 278.5 jit_solution(12034980832319321539)
XLA Ops:
  6.5 0.0 copy-start.1
  6.5 0.0 all-gather.6.cloned.1.call-start
  6.5 0.8 copy.7
  7.3 1.2 reduce-precision_select_fusion
  8.5 0.1 broadcast_in_dim.15
  8.6 0.7 fusion
  9.3 0.0 all-gather.6.cloned.1.call-update
  9.3 0.0 all-gather.8.cloned.1.call-start
  9.3 0.9 pad_maximum_fusion
  10.2 0.0 all-gather.8.cloned.1.call-update
  10.3 0.0 all-gather.10.cloned.1.call-start
  10.3 1.8 collective-permute-start
  12.1 0.0 collective-permute-done
  12.1 0.0 copy-start
  12.1 0.9 copy-done
  13.0 0.0 all-gather.10.cloned.1.call-update
  13.0 0.0 copy-done.1
  13.0 0.7 reshape_reshape.3.refs_2_
  13.7 0.5 multiply_add_fusion.refs_0_.refs_1_
  14.2 0.6 multiply_add_fusion.1.refs_0_
  14.8 62.0 %all-gather.6.cloned.1.call-done = f32[32,2,136,128]{3,2,1,0:T(8,128)} async-done(((f32[1,2,136,128]{3,2,1,0:T(8,128)}), f32[32,2,136,128]{3,2,1,0:T(8,128)}) %all-gather.6.cloned.1.call-update) | async-done | bytes 4456464 | tf_op jit(solution)/shard_map/all_gather | solution.py:276
  76.7 86.8 %factor_blocks.1 = (f32[1024,1024]{1,0:T(8,128)}, f32[8,128,128]{2,1,0:T(8,128)}) custom-call(f32[8,4,2,136,128]{4,3,2,1,0:T(8,128)} %bitcast.14), custom_call_target="tpu_custom_call" | custom-call | flops 40000000000 | bytes 9000000 | tf_op jit(solution)/shard_map/factor_blocks/pallas_call | solution.py:118
  163.6 0.0 all-gather.8.cloned.1.call-done
  163.6 23.6 %solve_panels.2.refs_4_ = f32[5,128,1024]{2,1,0:T(8,128)} custom-call(s32[5]{0:T(128)} %multiply_add_fusion.1.refs_0_, f32[4,5,2,136,128]{4,3,2,1,0:T(8,128)} %bitcast.15, f32[1024,1024]{1,0:T(8,128)} %get-tuple-element.7.refs_2_, f32[8,128,128]{2,1,0:T(8,128)} %get-tuple-element.8.refs_3_), custom_call_target="tpu_custom_call" | custom-call | flops 4000000000 | bytes 5000000 | tf_op jit(solution)/shard_map/solve_panels/pallas_call | solution.py:178
  187.2 8.7 %all-gather.10.cloned.1.call-done = f32[40,2,136,128]{3,2,1,0:T(8,128)} async-done(((f32[5,2,136,128]{3,2,1,0:T(8,128)}), f32[40,2,136,128]{3,2,1,0:T(8,128)}) %all-gather.10.cloned.1.call-update) | async-done | bytes 5570576 | tf_op jit(solution)/shard_map/all_gather | solution.py:288
  195.9 44.3 %solve_panels.3.refs_5_ = f32[10,128,1024]{2,1,0:T(8,128)} custom-call(s32[10]{0:T(128)} %multiply_add_fusion.refs_0_.refs_1_, f32[8,5,2,136,128]{4,3,2,1,0:T(8,128)} %bitcast.13, f32[1024,1024]{1,0:T(8,128)} %get-tuple-element.7.refs_2_, f32[8,128,128]{2,1,0:T(8,128)} %get-tuple-element.8.refs_3_), custom_call_target="tpu_custom_call" | custom-call | flops 8000000000 | bytes 10000000 | tf_op jit(solution)/shard_map/solve_panels/pallas_call | solution.py:178
  240.2 31.8 %update_tiles.1 = f32[5,10,128,128]{3,2,1,0:T(8,128)} custom-call(s32[5]{0:T(128)} %multiply_add_fusion.1.refs_0_, s32[10]{0:T(128)} %multiply_add_fusion.refs_0_.refs_1_, s32[50]{0:T(128)} %reshape_reshape.3.refs_2_, f32[5,10,128,128]{3,2,1,0:T(8,128)} %bitcast.11, f32[5,128,1024]{2,1,0:T(8,128)} %solve_panels.2.refs_4_, f32[10,128,1024]{2,1,0:T(8,128)} %solve_panels.3.refs_5_), custom_call_target="tpu_custom_call" | custom-call | tf_op jit(solution)/shard_map/update_tiles/pallas_call | solution.py:236
  (2 shorter events, 0.0 us)
Async XLA Ops:
  6.5 6.5 %copy-start.1 = (s32[5,1,10,1]{2,3,1,0:T(1,128)S(1)}, s32[5,1,10,1]{2,3,1,0:T(1,128)}, u32[]{:S(2)}) copy-start(s32[5,1,10,1]{2,3,1,0:T(1,128)} %param.3) | copy-start | bytes 604
  6.5 70.2 %all-gather.6.cloned.1.call-start = ((), (), s32[]{:S(2)}) async-start(), calls=%async_computation | async-start | bytes 4595712 | tf_op jit(solution)/shard_map/all_gather | solution.py:276
  9.3 154.3 %all-gather.8.cloned.1.call-start = ((), (), s32[]{:S(2)}) async-start(), calls=%async_computation.1 | async-start | bytes 3481600 | tf_op jit(solution)/shard_map/all_gather | solution.py:287
  10.3 185.6 %all-gather.10.cloned.1.call-start = ((), (), s32[]{:S(2)}) async-start(), calls=%async_computation.2 | async-start | bytes 6266880 | tf_op jit(solution)/shard_map/all_gather | solution.py:288
  10.3 1.8 collective-permute-start
  12.1 0.9 copy-start
Sparse Core Ops, SparseCore 0:
  10.2 66.5 all-gather.5
  78.3 24.9 all-gather.7
  105.5 90.4 all-gather.9

commit v2 on v1

v2 whole, which is shorter than its diff:
```python
import jax
import jax.numpy as jnp
from jax import lax
from jax.experimental import pallas as pl
from jax.experimental.pallas import tpu as pltpu
from jax.sharding import PartitionSpec as P

PT = 4
MICRO = 16
NT_DIMS = (((1,), (1,)), ((), ()))
TN_DIMS = (((0,), (0,)), ((), ()))


def dot_nt(a, b):
    return lax.dot_general(
        a, b, NT_DIMS, precision=lax.Precision.HIGHEST, preferred_element_type=jnp.float32
    )


def dot_nt_coarse(a, b):
    return lax.dot_general(
        a.astype(jnp.bfloat16),
        b.astype(jnp.bfloat16),
        NT_DIMS,
        preferred_element_type=jnp.float32,
    )


def split(value):
    high = value.astype(jnp.bfloat16)
    return high, (value - high.astype(jnp.float32)).astype(jnp.bfloat16)


def dot_bf16(a, b):
    return lax.dot_general(a, b, NT_DIMS, preferred_element_type=jnp.float32)


def dot_pairs(a, b):
    return dot_bf16(a[0], b[0]) + (dot_bf16(a[0], b[1]) + dot_bf16(a[1], b[0]))


def factor_tile(start, work_ref, low_ref, inv_ref):
    tile = start.shape[0]
    lane = lax.broadcasted_iota(jnp.int32, (tile, tile), 1)
    sub = lax.broadcasted_iota(jnp.int32, (tile, tile), 0)
    work_ref[:, :tile] = start
    work_ref[:, tile:] = (lane == sub).astype(jnp.float32)
    lane8 = lax.broadcasted_iota(jnp.int32, (MICRO, tile), 1)
    sub8 = lax.broadcasted_iota(jnp.int32, (MICRO, tile), 0)

    def micro(p, carry):
        base = pl.multiple_of(p * MICRO, MICRO)
        both = work_ref[pl.ds(base, MICRO), :]
        turned = pltpu.roll(both[:, :tile], lax.rem(tile - base, tile), 1)
        s = {}
        for k in range(MICRO):
            for q in range(k + 1):
                s[k, q] = jnp.broadcast_to(turned[k : k + 1, q : q + 1], (1, tile))
        rows = [both[k : k + 1, :tile] for k in range(MICRO)]
        more = [both[k : k + 1, tile:] for k in range(MICRO)]
        for q in range(MICRO):
            d = s[q, q]
            r = lax.rsqrt(d)
            r = r * (1.5 - 0.5 * d * r * r)
            rows[q] = rows[q] * r
            more[q] = more[q] * r
            low = {k: s[k, q] * r for k in range(q + 1, MICRO)}
            for k in range(q + 1, MICRO):
                for m in range(q + 1, k + 1):
                    s[k, m] = s[k, m] - low[k] * low[m]
                rows[k] = rows[k] - low[k] * rows[q]
                more[k] = more[k] - low[k] * more[q]
        upper = jnp.where(lane8 >= base + sub8, jnp.concatenate(rows, axis=0), 0.0)
        extra = jnp.concatenate(more, axis=0)
        low_ref[pl.ds(base, MICRO), :] = upper
        inv_ref[pl.ds(base, MICRO), :] = extra
        work_ref[...] -= lax.dot_general(
            upper,
            jnp.concatenate([upper, extra], axis=1),
            TN_DIMS,
            precision=lax.Precision.HIGHEST,
            preferred_element_type=jnp.float32,
        )
        return carry

    lax.fori_loop(0, tile // MICRO, micro, 0)


def factor_kernel(step, col_count, tile, grid_ref, *refs):
    if step:
        before_ref, low_ref, inv_ref, work_ref, up_ref = refs
    else:
        low_ref, inv_ref, work_ref, up_ref = refs
    first = step * PT
    count = 2 * PT - first
    lane = lax.broadcasted_iota(jnp.int32, (tile, tile), 1)
    sub = lax.broadcasted_iota(jnp.int32, (tile, tile), 0)

    def span(i, j=None):
        return slice(i * tile, (i + 1 if j is None else j) * tile)

    for i in range(count):
        for j in range(PT):
            if j > i:
                low_ref[span(i), span(j)] = jnp.zeros((tile, tile), jnp.float32)
                continue
            where = (first + i, (first + j) % col_count, j // col_count)
            piece = grid_ref[(*where, slice(0, tile))]
            if i == j:
                kept = jnp.where(lane <= sub, piece, 0.0)
                piece = kept + jnp.where(lane < sub, piece, 0.0).T
            if step:
                left = before_ref[span(PT + i), :]
                right = before_ref[span(PT + j), :]
                mark = grid_ref[(*where, slice(tile, tile + 1))]
                piece = piece - jnp.where(mark > 0.5, dot_nt_coarse(left, right), dot_nt(left, right))
            low_ref[span(i), span(j)] = piece
    for t in range(PT):
        factor_tile(low_ref[span(t), span(t)], work_ref, up_ref, inv_ref.at[t])
        low_ref[span(t), span(t)] = up_ref[...].T
        if t + 1 < count:
            solved = dot_nt(low_ref[span(t + 1, count), span(t)], inv_ref[t])
            low_ref[span(t + 1, count), span(t)] = solved
            for u in range(t + 1, PT):
                low_ref[span(u, count), span(u)] -= dot_nt(
                    low_ref[span(u, count), span(t)], low_ref[span(u), span(t)]
                )


def factor_blocks(step, grid, *before):
    col_count = grid.shape[1]
    tile = grid.shape[4]
    count = 2 * PT - step * PT
    vmem = pl.BlockSpec(memory_space=pltpu.VMEM)
    return pl.pallas_call(
        lambda *refs: factor_kernel(step, col_count, tile, *refs),
        out_shape=(
            jax.ShapeDtypeStruct((count * tile, PT * tile), jnp.float32),
            jax.ShapeDtypeStruct((PT, tile, tile), jnp.float32),
        ),
        in_specs=[vmem] * (1 + len(before)),
        out_specs=(vmem, vmem),
        scratch_shapes=[
            pltpu.VMEM((tile, 2 * tile), jnp.float32),
            pltpu.VMEM((tile, tile), jnp.float32),
        ],
        cost_estimate=pl.CostEstimate(flops=20_000_000_000, bytes_accessed=9_000_000, transcendentals=0),
        name="factor_blocks",
    )(grid, *before)


def solve_kernel(tile, groups, ids_ref, order_ref, panel_ref, low0_ref, inv0_ref, low1_ref, inv1_ref,
                 high_ref, rest_ref, low_h, low_l, inv_h, inv_l):
    count = 2 * PT
    width = PT * tile
    rows = panel_ref.shape[1]
    col_count = panel_ref.shape[0]
    group = pl.program_id(0)

    def span(i, j=None):
        return slice(i * tile, (i + 1 if j is None else j) * tile)

    @pl.when(group == 0)
    def _():
        for i in range(count):
            low_h[span(i), :width], low_l[span(i), :width] = split(low0_ref[span(i), :])
        for i in range(PT):
            at = PT + i
            low_h[span(at), width:], low_l[span(at), width:] = split(low1_ref[span(i), :])
            low_h[span(i), width:] = jnp.zeros((tile, width), jnp.bfloat16)
            low_l[span(i), width:] = jnp.zeros((tile, width), jnp.bfloat16)
            inv_h[i], inv_l[i] = split(inv0_ref[i])
            inv_h[at], inv_l[at] = split(inv1_ref[i])

    def flat(value):
        return value.reshape(rows * tile, tile)

    for t in range(count):
        first = t // PT * PT
        slot = t // col_count
        owner = order_ref[t]
        value = flat(panel_ref[owner, :, slot, :tile, :])
        if first:
            left = (high_ref[0, :, :width], rest_ref[0, :, :width])
            right = (low_h[span(t), :width], low_l[span(t), :width])
            coarse = dot_bf16(left[0], right[0])
            exact = coarse + (dot_bf16(left[0], right[1]) + dot_bf16(left[1], right[0]))
            mark = panel_ref[owner, :, slot, tile : tile + 1, :]
            mark = flat(jnp.broadcast_to(mark, (rows, tile, tile)))
            value = value - jnp.where(mark > 0.5, coarse, exact)
        if t > first:
            value = value - dot_pairs(
                (high_ref[0, :, span(first, t)], rest_ref[0, :, span(first, t)]),
                (low_h[span(t), span(first, t)], low_l[span(t), span(first, t)]),
            )
        high_ref[0, :, span(t)], rest_ref[0, :, span(t)] = split(
            dot_pairs(split(value), (inv_h[t], inv_l[t]))
        )

    row = ids_ref[group]

    @pl.when(row < count)
    def _():
        base = pl.multiple_of(jnp.minimum(row, count - 1) * tile, tile)
        high_ref[0, :tile, :] = low_h[pl.ds(base, tile), :]
        rest_ref[0, :tile, :] = low_l[pl.ds(base, tile), :]


def solve_panels(ids, order, panels, factors, groups):
    col_count = panels.shape[0] // groups
    _, rows, slots, height, tile = panels.shape
    count = 2 * PT
    full = count * tile
    keep = lambda n: (lambda g, *refs: (0,) * n)
    out_spec = pl.BlockSpec((1, rows * tile, full), lambda g, *refs: (g, 0, 0))
    out_shape = jax.ShapeDtypeStruct((groups, rows * tile, full), jnp.bfloat16)
    return pl.pallas_call(
        lambda *refs: solve_kernel(tile, groups, *refs),
        grid_spec=pltpu.PrefetchScalarGridSpec(
            num_scalar_prefetch=2,
            grid=(groups,),
            in_specs=[
                pl.BlockSpec((col_count, rows, slots, height, tile), lambda g, *refs: (g, 0, 0, 0, 0))
            ]
            + [pl.BlockSpec(f.shape, keep(len(f.shape))) for f in factors],
            out_specs=(out_spec, out_spec),
            scratch_shapes=[
                pltpu.VMEM((full, full), jnp.bfloat16),
                pltpu.VMEM((full, full), jnp.bfloat16),
                pltpu.VMEM((count, tile, tile), jnp.bfloat16),
                pltpu.VMEM((count, tile, tile), jnp.bfloat16),
            ],
        ),
        out_shape=(out_shape, out_shape),
        compiler_params=pltpu.CompilerParams(vmem_limit_bytes=56 * 1024 * 1024),
        cost_estimate=pl.CostEstimate(
            flops=groups * 4_000_000_000, bytes_accessed=groups * 6_000_000, transcendentals=0
        ),
        name="solve_panels",
    )(ids, order, panels, *factors)


def update_kernel(tile, groups, rows_ref, cols_ref, marks_ref, raw_ref, left_h, left_l, right_h, right_l, out_ref):
    count = 2 * PT
    b = pl.program_id(0)
    j = cols_ref[b]
    base = pl.multiple_of(jnp.minimum(j, count - 1) * tile, tile)
    at = pl.multiple_of(b // groups * tile, tile)
    group = b % groups

    def rounded(value):
        return value.astype(jnp.bfloat16).astype(jnp.float32)

    def tile_row(a):
        i = rows_ref[a]
        mark = marks_ref[a * pl.num_programs(0) + b]
        mine = slice(a * tile, (a + 1) * tile)

        @pl.when(i < j)
        def _():
            out_ref[a, 0] = jnp.zeros((tile, tile), jnp.float32)

        @pl.when((i >= j) & (j < count))
        def _():
            high = left_h[0, mine, pl.ds(base, tile)].astype(jnp.float32)
            rest = left_l[0, mine, pl.ds(base, tile)].astype(jnp.float32)
            out_ref[a, 0] = high + jnp.where(mark == 1, 0.0, rest)

        @pl.when((i >= j) & (j >= count) & (mark == 1))
        def _():
            other = right_h[group, pl.ds(at, tile), :]
            out_ref[a, 0] = rounded(rounded(raw_ref[a, 0]) - dot_bf16(left_h[0, mine, :], other))

        @pl.when((i >= j) & (j >= count) & (mark != 1))
        def _():
            high = right_h[group, pl.ds(at, tile), :]
            rest = right_l[group, pl.ds(at, tile), :]
            out_ref[a, 0] = raw_ref[a, 0] - dot_pairs(
                (left_h[0, mine, :], left_l[0, mine, :]), (high, rest)
            )

    for a in range(raw_ref.shape[0]):
        tile_row(a)


def update_tiles(row_ids, col_ids, marks, tiles, left, right):
    rows, cols, tile, _ = tiles.shape
    groups = right[0].shape[0]
    whole = lambda b, *refs: (0, 0, 0)
    each = pl.BlockSpec((rows, 1, tile, tile), lambda b, *refs: (0, b, 0, 0))
    return pl.pallas_call(
        lambda *refs: update_kernel(tile, groups, *refs),
        grid_spec=pltpu.PrefetchScalarGridSpec(
            num_scalar_prefetch=3,
            grid=(cols,),
            in_specs=[each] + [pl.BlockSpec(v.shape, whole) for v in (*left, *right)],
            out_specs=each,
        ),
        out_shape=jax.ShapeDtypeStruct(tiles.shape, jnp.float32),
        compiler_params=pltpu.CompilerParams(vmem_limit_bytes=60 * 1024 * 1024),
        name="update_tiles",
    )(row_ids, col_ids, marks.reshape(-1), tiles, *left, *right)


def on_device(matrix, flags):
    row_count = lax.axis_size("row")
    col_count = lax.axis_size("col")
    row_index = lax.axis_index("row")
    col_index = lax.axis_index("col")
    tile_rows = matrix.shape[0]
    tile_cols = matrix.shape[2]
    tile = matrix.shape[4]
    count = 2 * PT
    slots = count // col_count
    groups = row_count // col_count
    tiles = matrix.reshape(tile_rows, tile_cols, tile, tile)
    marks = flags.reshape(tile_rows, tile_cols)
    row_ids = jnp.arange(tile_rows, dtype=jnp.int32) * row_count + row_index
    col_ids = jnp.arange(tile_cols, dtype=jnp.int32) * col_count + col_index

    head = tiles[:, :slots]
    head_marks = (marks[:, :slots] == 1)[:, :, None, None]
    stored = jnp.where(head_marks, lax.reduce_precision(head, 8, 7), head)
    tags = jnp.broadcast_to(head_marks.astype(jnp.float32), (tile_rows, slots, 8, tile))
    payload = jnp.concatenate([stored, tags], axis=2)

    half = max(slots // 2, 1)
    grids = []
    for step in range(2 if slots > 1 else 1):
        piece = payload[0, step * half : (step + 1) * half]
        grid = lax.all_gather(piece, ("row", "col"))
        grids.append(grid.reshape(row_count, col_count, half, tile + 8, tile)[:count])
    low0, inv0 = factor_blocks(0, grids[0])
    low1, inv1 = factor_blocks(1, grids[-1], low0)
    factors = (low0, inv0, low1, inv1)

    perm = []
    for h in range(groups):
        for u in range(col_count):
            for v in range(col_count):
                source = (h * col_count + u) * col_count + v
                perm.append((source, (h * col_count + v) * col_count + u))
    swapped = lax.ppermute(payload, ("row", "col"), perm)
    pieces = [payload]
    for shift in range(1, col_count):
        ring = [(q, (q + shift) % col_count) for q in range(col_count)]
        pieces.append(lax.ppermute(payload, "col", ring))
    own = jnp.stack(pieces)
    across = lax.all_gather(swapped, "row")

    columns = jnp.arange(count, dtype=jnp.int32)
    turned = (col_index - columns + count * col_count) % col_count
    left = solve_panels(row_ids[:1], turned, own, factors, 1)
    right = solve_panels(col_ids[:groups], columns % col_count, across, factors, groups)
    out = update_tiles(row_ids, col_ids, marks, tiles, left, right)
    return out.reshape(matrix.shape)


def solution(mesh):
    return jax.shard_map(
        on_device,
        mesh=mesh,
        in_specs=(P(None, "row", None, "col", None, None), P(None, "row", None, "col")),
        out_specs=P(None, "row", None, "col", None, None),
        check_vma=False,
    )
```

time: 281 us -> 264 us (0.940)
  Pallas kernels: 187 us -> 116 us
  waiting for transfers between devices: 70.8 us -> 97.8 us
  starting transfers between devices: 1.85 us -> 26.9 us
  other arithmetic: 3.88 us -> 7.03 us
    pallas_call x4 -> x5, Pallas kernels: 187 us -> 116 us  [the longest x2 71.5 us: factor_blocks(): pl.pallas_call(lambda *refs: factor_kernel(step, col_count, tile, *refs),...]
    all_gather x2, waiting for transfers between devices: 62 us -> 23.5 us  [on_device(): grid = lax.all_gather(piece, ('row', 'col'))]
    all_gather x1, waiting for transfers between devices: 8.72 us -> 42.5 us  [on_device(): across = lax.all_gather(swapped, 'row')]
    ppermute x0 -> x3, waiting for transfers between devices: none -> 31 us  [on_device(): pieces.append(lax.ppermute(payload, 'col', ring))]
    ppermute x0 -> x3, starting transfers between devices: none -> 26.1 us  [on_device(): pieces.append(lax.ppermute(payload, 'col', ring))]
    another operation x0 -> x2, other arithmetic: none -> 3.02 us  [on_device(): own = jnp.stack(pieces)]
  transfers between devices with their start and end apart: 4 -> 7, of which waited for: 2 -> 6; matrix products, arithmetic and copies ran while one was open for 1% -> 2% of each run, Pallas kernels for 40% -> 32%
where the time goes in v2:
time: 264 us
  Pallas kernels  116 us (44%)
  waiting for transfers between devices  97.8 us (37%)
  starting transfers between devices  26.9 us (10%)
  between operations  13.2 us (5%)
  other arithmetic  7.03 us (3%)
    pallas_call x2, Pallas kernels, factor_blocks(): pl.pallas_call(lambda *refs: factor_kernel(step, col_count, tile, *refs),...  71.5 us
    all_gather x1, waiting for transfers between devices, on_device(): across = lax.all_gather(swapped, 'row')  42.5 us
    pallas_call x2, Pallas kernels, solve_panels(): pl.pallas_call(lambda *refs: solve_kernel(tile, groups, *refs), grid_spec...  31.7 us
    ppermute x3, waiting for transfers between devices, on_device(): pieces.append(lax.ppermute(payload, 'col', ring))  31 us
    ppermute x3, starting transfers between devices, on_device(): pieces.append(lax.ppermute(payload, 'col', ring))  26.1 us
    all_gather x2, waiting for transfers between devices, on_device(): grid = lax.all_gather(piece, ('row', 'col'))  23.5 us
    pallas_call x1, Pallas kernels, update_tiles(): pl.pallas_call(lambda *refs: update_kernel(tile, groups, *refs), grid_spe...  13.1 us
  transfers between devices with their start and end apart: 7, of which 6 were waited for; matrix products, arithmetic and copies ran while one was open for 2% of the time, Pallas kernels for 32%

profile of v2, /device:TPU:0, one launch (start us, length us, event | category | flops | bytes accessed | tf_op | source)
XLA Modules:
  0.0 263.5 jit_solution(1184490743661970922)
XLA Ops:
  6.5 0.0 copy-start.1
  6.5 0.0 all-gather.5.cloned.1.call-start
  6.5 0.8 copy.9
  7.3 1.2 reduce-precision_select_fusion
  8.5 0.1 broadcast_in_dim.15
  8.6 0.7 fusion.1
  9.2 0.0 all-gather.5.cloned.1.call-update
  9.3 0.0 all-gather.7.cloned.1.call-start
  9.3 0.7 all-gather.7.cloned.1.call-update
  10.0 0.0 all-gather.9.cloned.1.call-start
  10.1 0.1 fusion.3
  10.2 0.7 collective-permute-start.3
  10.9 0.0 collective-permute-done.3
  10.9 0.0 copy-start
  10.9 0.9 copy-done
  11.8 0.0 all-gather.9.cloned.1.call-update
  11.8 19.2 %collective-permute-start = (f32[5,2,136,128]{3,2,1,0:T(8,128)S(1)}, f32[5,2,136,128]{3,2,1,0:T(8,128)S(1)}, u32[]{:S(2)}, u32[]{:S(2)}) collective-permute-start(f32[5,2,136,128]{3,2,1,0:T(8,128)S(1)} %get-tuple-element.26), channel_id=1, source_target_pairs={{0,1},{1,2},{2,3},{3,0},{4,5},{5,6},{6,7},{7,4},{8,9},{9,10},{10,1... | collective-permute-start | bytes 2088968 | tf_op jit(solution)/shard_map/ppermute | solution.py:347
  31.0 5.5 %collective-permute-start.1 = (f32[5,2,136,128]{3,2,1,0:T(8,128)S(1)}, f32[5,2,136,128]{3,2,1,0:T(8,128)S(1)}, u32[]{:S(2)}, u32[]{:S(2)}) collective-permute-start(f32[5,2,136,128]{3,2,1,0:T(8,128)S(1)} %get-tuple-element.26), channel_id=1, source_target_pairs={{0,2},{1,3},{2,0},{3,1},{4,6},{5,7},{6,4},{7,5},{8,10},{9,11},{10,... | collective-permute-start | bytes 2088968 | tf_op jit(solution)/shard_map/ppermute | solution.py:347
  36.5 1.4 collective-permute-start.2
  37.9 0.0 copy-done.1
  37.9 0.6 reshape_reshape.3.refs_2_
  38.6 0.5 and_select_fusion.1.refs_1_
  39.1 0.5 multiply_add_fusion.refs_1_
  39.6 0.5 and_select_fusion.refs_1_
  40.2 0.5 multiply_add_fusion.1.refs_0_
  40.7 11.8 %collective-permute-done = f32[5,2,136,128]{3,2,1,0:T(8,128)S(1)} collective-permute-done((f32[5,2,136,128]{3,2,1,0:T(8,128)S(1)}, f32[5,2,136,128]{3,2,1,0:T(8,128)S(1)}, u32[]{:S(2)}, u32[]{:S(2)}) %collective-permute-start) | collective-permute-done | bytes 696352 | tf_op jit(solution)/shard_map/ppermute | solution.py:347
  52.5 1.5 collective-permute-done.1
  54.0 17.7 %collective-permute-done.2 = f32[5,2,136,128]{3,2,1,0:T(8,128)} collective-permute-done((f32[5,2,136,128]{3,2,1,0:T(8,128)S(1)}, f32[5,2,136,128]{3,2,1,0:T(8,128)}, u32[]{:S(2)}, u32[]{:S(2)}) %collective-permute-start.2) | collective-permute-done | bytes 696352 | tf_op jit(solution)/shard_map/ppermute | solution.py:347
  71.7 2.9 %pad_maximum_fusion.refs_2_ = f32[4,5,2,136,128]{4,3,2,1,0:T(8,128)} fusion(f32[1,5,2,136,128]{4,3,2,1,0:T(8,128)} %bitcast.4, f32[1,5,2,136,128]{4,3,2,1,0:T(8,128)S(1)} %bitcast.20, f32[1,5,2,136,128]{4,3,2,1,0:T(8,128)S(1)} %bitcast.19, f32[1,5,2,136,128]{4,3,2,1,0:T(8,128)S(1)} %get-tuple-element.25), kind=kLoop, calls=%fused_computation | loop fusion | flops 2088960 | bytes 5570560 | tf_op jit(solution)/shard_map/stack | solution.py:348
  74.6 0.2 all-gather.5.cloned.1.call-done
  74.8 35.6 %factor_blocks.2 = (f32[1024,512]{1,0:T(8,128)}, f32[4,128,128]{2,1,0:T(8,128)}) custom-call(f32[8,4,1,136,128]{4,3,2,1,0:T(8,128)} %bitcast.25), custom_call_target="tpu_custom_call" | custom-call | flops 20000000000 | bytes 9000000 | tf_op jit(solution)/shard_map/factor_blocks/pallas_call | solution.py:135
  110.4 23.3 %all-gather.7.cloned.1.call-done = f32[32,1,136,128]{3,2,1,0:T(8,128)} async-done(((f32[1,1,136,128]{3,2,1,0:T(8,128)}), f32[32,1,136,128]{3,2,1,0:T(8,128)}) %all-gather.7.cloned.1.call-update) | async-done | bytes 2228240 | tf_op jit(solution)/shard_map/all_gather | solution.py:331
  133.8 35.9 %factor_blocks.3 = (f32[512,512]{1,0:T(8,128)}, f32[4,128,128]{2,1,0:T(8,128)}) custom-call(f32[8,4,1,136,128]{4,3,2,1,0:T(8,128)} %bitcast.26, f32[1024,512]{1,0:T(8,128)} %get-tuple-element.13.refs_1_.refs_3_), custom_call_target="tpu_custom_call" | custom-call | flops 20000000000 | bytes 9000000 | tf_op jit(solution)/shard_map/factor_blocks/pallas_call | solution.py:135
  169.7 12.6 %solve_panels.2 = (bf16[1,640,1024]{2,1,0:T(8,128)(2,1)}, bf16[1,640,1024]{2,1,0:T(8,128)(2,1)}) custom-call(s32[1]{0:T(128)} %bitcast.23, s32[8]{0:T(128)} %and_select_fusion.1.refs_1_, f32[4,5,2,136,128]{4,3,2,1,0:T(8,128)} %pad_maximum_fusion.refs_2_, f32[1024,512]{1,0:T(8,128)} %get-tuple-element.13.refs_1_.refs_3_, ...), custom_call_target="tpu_custom_call" | custom-call | flops 4000000000 | bytes 6000000 | tf_op jit(solution)/shard_map/solve_panels/pallas_call | solution.py:217
  182.2 42.5 %all-gather.9.cloned.1.call-done = f32[40,2,136,128]{3,2,1,0:T(8,128)} async-done(((f32[5,2,136,128]{3,2,1,0:T(8,128)}), f32[40,2,136,128]{3,2,1,0:T(8,128)}) %all-gather.9.cloned.1.call-update) | async-done | bytes 5570576 | tf_op jit(solution)/shard_map/all_gather | solution.py:349
  224.7 19.2 %solve_panels.3 = (bf16[2,640,1024]{2,1,0:T(8,128)(2,1)}, bf16[2,640,1024]{2,1,0:T(8,128)(2,1)}) custom-call(s32[2]{0:T(128)} %bitcast.22, s32[8]{0:T(128)} %and_select_fusion.refs_1_, f32[8,5,2,136,128]{4,3,2,1,0:T(8,128)} %bitcast.24, f32[1024,512]{1,0:T(8,128)} %get-tuple-element.13.refs_1_.refs_3_, f32[4,128,128]{2,1,0:T(8,128)} %get-tuple-element.14.refs_4_, ...), custom_call_target="tpu_custom_call" | custom-call | flops 8000000000 | bytes 12000000 | tf_op jit(solution)/shard_map/solve_panels/pallas_call | solution.py:217
  243.9 13.1 %update_tiles.1 = f32[5,10,128,128]{3,2,1,0:T(8,128)} custom-call(s32[5]{0:T(128)} %multiply_add_fusion.1.refs_0_, s32[10]{0:T(128)} %multiply_add_fusion.refs_1_, s32[50]{0:T(128)} %reshape_reshape.3.refs_2_, f32[5,10,128,128]{3,2,1,0:T(8,128)} %bitcast.18, bf16[1,640,1024]{2,1,0:T(8,128)(2,1)} %get-tuple-element.17.refs_4_, ...), custom_call_target="tpu_custom_call" | custom-call | tf_op jit(solution)/shard_map/update_tiles/pallas_call | solution.py:291
  (2 shorter events, 0.0 us)
Async XLA Ops:
  6.5 31.4 %copy-start.1 = (s32[5,1,10,1]{2,3,1,0:T(1,128)S(1)}, s32[5,1,10,1]{2,3,1,0:T(1,128)}, u32[]{:S(2)}) copy-start(s32[5,1,10,1]{2,3,1,0:T(1,128)} %param.3) | copy-start | bytes 604
  6.5 68.3 %all-gather.5.cloned.1.call-start = ((), (), s32[]{:S(2)}) async-start(), calls=%async_computation | async-start | bytes 2297856 | tf_op jit(solution)/shard_map/all_gather | solution.py:331
  9.3 124.5 %all-gather.7.cloned.1.call-start = ((), (), s32[]{:S(2)}) async-start(), calls=%async_computation.1 | async-start | bytes 2297856 | tf_op jit(solution)/shard_map/all_gather | solution.py:331
  10.0 214.7 %all-gather.9.cloned.1.call-start = ((), (), s32[]{:S(2)}) async-start(), calls=%async_computation.2 | async-start | bytes 6266880 | tf_op jit(solution)/shard_map/all_gather | solution.py:349
  10.2 0.7 collective-permute-start.3
  10.9 0.9 copy-start
  11.8 40.7 %collective-permute-start = (f32[5,2,136,128]{3,2,1,0:T(8,128)S(1)}, f32[5,2,136,128]{3,2,1,0:T(8,128)S(1)}, u32[]{:S(2)}, u32[]{:S(2)}) collective-permute-start(f32[5,2,136,128]{3,2,1,0:T(8,128)S(1)} %get-tuple-element.26), channel_id=1, source_target_pairs={{0,1},{1,2},{2,3},{3,0},{4,5},{5,6},{6,7},{7,4},{8,9},{9,10},{10,1... | collective-permute-start | bytes 2088968 | tf_op jit(solution)/shard_map/ppermute | solution.py:347
  31.0 23.0 %collective-permute-start.1 = (f32[5,2,136,128]{3,2,1,0:T(8,128)S(1)}, f32[5,2,136,128]{3,2,1,0:T(8,128)S(1)}, u32[]{:S(2)}, u32[]{:S(2)}) collective-permute-start(f32[5,2,136,128]{3,2,1,0:T(8,128)S(1)} %get-tuple-element.26), channel_id=1, source_target_pairs={{0,2},{1,3},{2,0},{3,1},{4,6},{5,7},{6,4},{7,5},{8,10},{9,11},{10,... | collective-permute-start | bytes 2088968 | tf_op jit(solution)/shard_map/ppermute | solution.py:347
  36.5 35.1 %collective-permute-start.2 = (f32[5,2,136,128]{3,2,1,0:T(8,128)S(1)}, f32[5,2,136,128]{3,2,1,0:T(8,128)}, u32[]{:S(2)}, u32[]{:S(2)}) collective-permute-start(f32[5,2,136,128]{3,2,1,0:T(8,128)S(1)} %get-tuple-element.26), channel_id=1, source_target_pairs={{0,3},{1,0},{2,1},{3,2},{4,7},{5,4},{6,5},{7,6},{8,11},{9,8},{10,9... | collective-permute-start | bytes 2088968 | tf_op jit(solution)/shard_map/ppermute | solution.py:347
Sparse Core Ops, SparseCore 0:
  10.2 64.5 all-gather.4
  77.7 56.0 all-gather.6
  135.9 88.7 all-gather.8

commit v3 on v2

--- a/solution.py
+++ b/solution.py
@@ -104,7 +104,7 @@
             if j > i:
                 low_ref[span(i), span(j)] = jnp.zeros((tile, tile), jnp.float32)
                 continue
-            where = (first + i, (first + j) % col_count, j // col_count)
+            where = (first + i, (first + j) % col_count, (first + j) // col_count)
             piece = grid_ref[(*where, slice(0, tile))]
             if i == j:
                 kept = jnp.where(lane <= sub, piece, 0.0)
@@ -324,14 +324,10 @@
     tags = jnp.broadcast_to(head_marks.astype(jnp.float32), (tile_rows, slots, 8, tile))
     payload = jnp.concatenate([stored, tags], axis=2)
 
-    half = max(slots // 2, 1)
-    grids = []
-    for step in range(2 if slots > 1 else 1):
-        piece = payload[0, step * half : (step + 1) * half]
-        grid = lax.all_gather(piece, ("row", "col"))
-        grids.append(grid.reshape(row_count, col_count, half, tile + 8, tile)[:count])
-    low0, inv0 = factor_blocks(0, grids[0])
-    low1, inv1 = factor_blocks(1, grids[-1], low0)
+    grid = lax.all_gather(payload[0], ("row", "col"))
+    grid = grid.reshape(row_count, col_count, slots, tile + 8, tile)[:count]
+    low0, inv0 = factor_blocks(0, grid)
+    low1, inv1 = factor_blocks(1, grid, low0)
     factors = (low0, inv0, low1, inv1)
 
     perm = []

time: 264 us -> 216 us (0.82)
  waiting for transfers between devices: 97.8 us -> 46.2 us
    all_gather x1, waiting for transfers between devices: 42.5 us -> 5.51 us  [on_device(): across = lax.all_gather(swapped, 'row')]
    all_gather x2 -> x1, waiting for transfers between devices: 23.5 us -> 4.7 us  [on_device(): grid = lax.all_gather(payload[0], ('row', 'col'))]
    ppermute x3, waiting for transfers between devices: 31 us -> 36 us  [on_device(): pieces.append(lax.ppermute(payload, 'col', ring))]
  transfers between devices with their start and end apart: 7 -> 6, of which waited for: 6 -> 5; matrix products, arithmetic and copies ran while one was open for 2% -> 3% of each run, Pallas kernels for 32% -> 40%
where the time goes in v3:
time: 216 us; the launch traced here: 215 us
  Pallas kernels  118 us (55%)
  waiting for transfers between devices  46.2 us (21%)
  starting transfers between devices  28.4 us (13%)
  between operations  13.4 us (6%)
  other arithmetic  7.05 us (3%)
  local copies, waits for them, and re-layouts  2.36 us (1%)
    pallas_call x2, Pallas kernels, factor_blocks(): pl.pallas_call(lambda *refs: factor_kernel(step, col_count, tile, *refs),...  72.9 us
    ppermute x3, waiting for transfers between devices, on_device(): pieces.append(lax.ppermute(payload, 'col', ring))  36 us
    pallas_call x2, Pallas kernels, solve_panels(): pl.pallas_call(lambda *refs: solve_kernel(tile, groups, *refs), grid_spec...  31.7 us
    ppermute x3, starting transfers between devices, on_device(): pieces.append(lax.ppermute(payload, 'col', ring))  27.7 us
    pallas_call x1, Pallas kernels, update_tiles(): pl.pallas_call(lambda *refs: update_kernel(tile, groups, *refs), grid_spe...  13.1 us
    all_gather x1, waiting for transfers between devices, on_device(): across = lax.all_gather(swapped, 'row')  5.51 us
    all_gather x1, waiting for transfers between devices, on_device(): grid = lax.all_gather(payload[0], ('row', 'col'))  4.7 us
  transfers between devices with their start and end apart: 6, of which 5 were waited for; matrix products, arithmetic and copies ran while one was open for 3% of the time, Pallas kernels for 40%

profile of v3, /device:TPU:0, one launch (start us, length us, event | category | flops | bytes accessed | tf_op | source)
XLA Modules:
  0.0 215.1 jit_solution(4545458247570303971)
XLA Ops:
  6.5 0.0 copy-start.1
  6.5 0.0 all-gather.4.cloned.1.call-start
  6.5 0.8 copy.7
  7.3 1.2 reduce-precision_select_fusion
  8.5 0.1 broadcast_in_dim.15
  8.6 0.7 fusion
  9.3 0.0 all-gather.4.cloned.1.call-update
  9.3 0.0 all-gather.6.cloned.1.call-start
  9.3 0.1 fusion.2
  9.4 0.7 collective-permute-start.3
  10.2 0.0 collective-permute-done.3
  10.2 0.0 copy-start
  10.2 0.9 copy-done
  11.0 0.0 all-gather.6.cloned.1.call-update
  11.1 19.9 %collective-permute-start = (f32[5,2,136,128]{3,2,1,0:T(8,128)S(1)}, f32[5,2,136,128]{3,2,1,0:T(8,128)S(1)}, u32[]{:S(2)}, u32[]{:S(2)}) collective-permute-start(f32[5,2,136,128]{3,2,1,0:T(8,128)S(1)} %get-tuple-element.24), channel_id=1, source_target_pairs={{0,1},{1,2},{2,3},{3,0},{4,5},{5,6},{6,7},{7,4},{8,9},{9,10},{10,1... | collective-permute-start | bytes 2088968 | tf_op jit(solution)/shard_map/ppermute | solution.py:343
  31.0 6.4 %collective-permute-start.1 = (f32[5,2,136,128]{3,2,1,0:T(8,128)S(1)}, f32[5,2,136,128]{3,2,1,0:T(8,128)S(1)}, u32[]{:S(2)}, u32[]{:S(2)}) collective-permute-start(f32[5,2,136,128]{3,2,1,0:T(8,128)S(1)} %get-tuple-element.24), channel_id=1, source_target_pairs={{0,2},{1,3},{2,0},{3,1},{4,6},{5,7},{6,4},{7,5},{8,10},{9,11},{10,... | collective-permute-start | bytes 2088968 | tf_op jit(solution)/shard_map/ppermute | solution.py:343
  37.3 1.4 collective-permute-start.2
  38.7 0.0 copy-done.1
  38.8 0.7 reshape_reshape.3.refs_2_
  39.4 0.6 and_select_fusion.refs_1_
  40.0 0.5 multiply_add_fusion.refs_1_
  40.5 0.6 and_select_fusion.1.refs_1_
  41.0 0.5 multiply_add_fusion.1.refs_0_
  41.6 12.7 %collective-permute-done = f32[5,2,136,128]{3,2,1,0:T(8,128)S(1)} collective-permute-done((f32[5,2,136,128]{3,2,1,0:T(8,128)S(1)}, f32[5,2,136,128]{3,2,1,0:T(8,128)S(1)}, u32[]{:S(2)}, u32[]{:S(2)}) %collective-permute-start) | collective-permute-done | bytes 696352 | tf_op jit(solution)/shard_map/ppermute | solution.py:343
  54.2 1.6 collective-permute-done.1
  55.8 21.7 %collective-permute-done.2 = f32[5,2,136,128]{3,2,1,0:T(8,128)} collective-permute-done((f32[5,2,136,128]{3,2,1,0:T(8,128)S(1)}, f32[5,2,136,128]{3,2,1,0:T(8,128)}, u32[]{:S(2)}, u32[]{:S(2)}) %collective-permute-start.2) | collective-permute-done | bytes 696352 | tf_op jit(solution)/shard_map/ppermute | solution.py:343
  77.5 2.9 %pad_maximum_fusion.refs_2_ = f32[4,5,2,136,128]{4,3,2,1,0:T(8,128)} fusion(f32[1,5,2,136,128]{4,3,2,1,0:T(8,128)} %bitcast.4, f32[1,5,2,136,128]{4,3,2,1,0:T(8,128)S(1)} %bitcast.19, f32[1,5,2,136,128]{4,3,2,1,0:T(8,128)S(1)} %bitcast.18, f32[1,5,2,136,128]{4,3,2,1,0:T(8,128)S(1)} %get-tuple-element.23), kind=kLoop, calls=%fused_computation | loop fusion | flops 2088960 | bytes 5570560 | tf_op jit(solution)/shard_map/stack | solution.py:344
  80.4 4.7 %all-gather.4.cloned.1.call-done = f32[32,2,136,128]{3,2,1,0:T(8,128)} async-done(((f32[1,2,136,128]{3,2,1,0:T(8,128)}), f32[32,2,136,128]{3,2,1,0:T(8,128)}) %all-gather.4.cloned.1.call-update) | async-done | bytes 4456464 | tf_op jit(solution)/shard_map/all_gather | solution.py:327
  85.1 36.3 %factor_blocks.2 = (f32[1024,512]{1,0:T(8,128)}, f32[4,128,128]{2,1,0:T(8,128)}) custom-call(f32[8,4,2,136,128]{4,3,2,1,0:T(8,128)} %bitcast.24), custom_call_target="tpu_custom_call" | custom-call | flops 20000000000 | bytes 9000000 | tf_op jit(solution)/shard_map/factor_blocks/pallas_call | solution.py:135
  121.4 36.6 %factor_blocks.3 = (f32[512,512]{1,0:T(8,128)}, f32[4,128,128]{2,1,0:T(8,128)}) custom-call(f32[8,4,2,136,128]{4,3,2,1,0:T(8,128)} %bitcast.25, f32[1024,512]{1,0:T(8,128)} %get-tuple-element.13.refs_1_.refs_3_), custom_call_target="tpu_custom_call" | custom-call | flops 20000000000 | bytes 9000000 | tf_op jit(solution)/shard_map/factor_blocks/pallas_call | solution.py:135
  158.0 12.6 %solve_panels.2 = (bf16[1,640,1024]{2,1,0:T(8,128)(2,1)}, bf16[1,640,1024]{2,1,0:T(8,128)(2,1)}) custom-call(s32[1]{0:T(128)} %bitcast.22, s32[8]{0:T(128)} %and_select_fusion.1.refs_1_, f32[4,5,2,136,128]{4,3,2,1,0:T(8,128)} %pad_maximum_fusion.refs_2_, f32[1024,512]{1,0:T(8,128)} %get-tuple-element.13.refs_1_.refs_3_, ...), custom_call_target="tpu_custom_call" | custom-call | flops 4000000000 | bytes 6000000 | tf_op jit(solution)/shard_map/solve_panels/pallas_call | solution.py:217
  170.6 5.5 %all-gather.6.cloned.1.call-done = f32[40,2,136,128]{3,2,1,0:T(8,128)} async-done(((f32[5,2,136,128]{3,2,1,0:T(8,128)}), f32[40,2,136,128]{3,2,1,0:T(8,128)}) %all-gather.6.cloned.1.call-update) | async-done | bytes 5570576 | tf_op jit(solution)/shard_map/all_gather | solution.py:345
  176.1 19.1 %solve_panels.3 = (bf16[2,640,1024]{2,1,0:T(8,128)(2,1)}, bf16[2,640,1024]{2,1,0:T(8,128)(2,1)}) custom-call(s32[2]{0:T(128)} %bitcast.21, s32[8]{0:T(128)} %and_select_fusion.refs_1_, f32[8,5,2,136,128]{4,3,2,1,0:T(8,128)} %bitcast.23, f32[1024,512]{1,0:T(8,128)} %get-tuple-element.13.refs_1_.refs_3_, f32[4,128,128]{2,1,0:T(8,128)} %get-tuple-element.14.refs_4_, ...), custom_call_target="tpu_custom_call" | custom-call | flops 8000000000 | bytes 12000000 | tf_op jit(solution)/shard_map/solve_panels/pallas_call | solution.py:217
  195.2 13.1 %update_tiles.1 = f32[5,10,128,128]{3,2,1,0:T(8,128)} custom-call(s32[5]{0:T(128)} %multiply_add_fusion.1.refs_0_, s32[10]{0:T(128)} %multiply_add_fusion.refs_1_, s32[50]{0:T(128)} %reshape_reshape.3.refs_2_, f32[5,10,128,128]{3,2,1,0:T(8,128)} %bitcast.17, bf16[1,640,1024]{2,1,0:T(8,128)(2,1)} %get-tuple-element.17.refs_4_, ...), custom_call_target="tpu_custom_call" | custom-call | tf_op jit(solution)/shard_map/update_tiles/pallas_call | solution.py:291
  (2 shorter events, 0.0 us)
Async XLA Ops:
  6.5 32.2 %copy-start.1 = (s32[5,1,10,1]{2,3,1,0:T(1,128)S(1)}, s32[5,1,10,1]{2,3,1,0:T(1,128)}, u32[]{:S(2)}) copy-start(s32[5,1,10,1]{2,3,1,0:T(1,128)} %param.3) | copy-start | bytes 604
  6.5 78.6 %all-gather.4.cloned.1.call-start = ((), (), s32[]{:S(2)}) async-start(), calls=%async_computation | async-start | bytes 4595712 | tf_op jit(solution)/shard_map/all_gather | solution.py:327
  9.3 166.8 %all-gather.6.cloned.1.call-start = ((), (), s32[]{:S(2)}) async-start(), calls=%async_computation.1 | async-start | bytes 6266880 | tf_op jit(solution)/shard_map/all_gather | solution.py:345
  9.4 0.7 collective-permute-start.3
  10.2 0.9 copy-start
  11.1 43.2 %collective-permute-start = (f32[5,2,136,128]{3,2,1,0:T(8,128)S(1)}, f32[5,2,136,128]{3,2,1,0:T(8,128)S(1)}, u32[]{:S(2)}, u32[]{:S(2)}) collective-permute-start(f32[5,2,136,128]{3,2,1,0:T(8,128)S(1)} %get-tuple-element.24), channel_id=1, source_target_pairs={{0,1},{1,2},{2,3},{3,0},{4,5},{5,6},{6,7},{7,4},{8,9},{9,10},{10,1... | collective-permute-start | bytes 2088968 | tf_op jit(solution)/shard_map/ppermute | solution.py:343
  31.0 24.9 %collective-permute-start.1 = (f32[5,2,136,128]{3,2,1,0:T(8,128)S(1)}, f32[5,2,136,128]{3,2,1,0:T(8,128)S(1)}, u32[]{:S(2)}, u32[]{:S(2)}) collective-permute-start(f32[5,2,136,128]{3,2,1,0:T(8,128)S(1)} %get-tuple-element.24), channel_id=1, source_target_pairs={{0,2},{1,3},{2,0},{3,1},{4,6},{5,7},{6,4},{7,5},{8,10},{9,11},{10,... | collective-permute-start | bytes 2088968 | tf_op jit(solution)/shard_map/ppermute | solution.py:343
  37.3 40.2 %collective-permute-start.2 = (f32[5,2,136,128]{3,2,1,0:T(8,128)S(1)}, f32[5,2,136,128]{3,2,1,0:T(8,128)}, u32[]{:S(2)}, u32[]{:S(2)}) collective-permute-start(f32[5,2,136,128]{3,2,1,0:T(8,128)S(1)} %get-tuple-element.24), channel_id=1, source_target_pairs={{0,3},{1,0},{2,1},{3,2},{4,7},{5,4},{6,5},{7,6},{8,11},{9,8},{10,9... | collective-permute-start | bytes 2088968 | tf_op jit(solution)/shard_map/ppermute | solution.py:343
Sparse Core Ops, SparseCore 0:
  10.2 74.9 all-gather.3
  87.3 88.7 all-gather.5
